TPU v7x, 32 devices: a whole 2x2x4 slice. The times are simulated.
32 devices in a mesh: ep: 4 (over z), fsdp: 4 (over x, core), tp: 2 (over y).
Axes of the slice: x: 2, y: 2, z: 4, core: 2. Of those that a mesh axis runs over, the one named last changes fastest.
Arguments:
- out_grad: bfloat16 [2048, 4096], P(('ep', 'fsdp')), may hold values from -1.5 to 1.5
- routes: int32 [2048, 2], P(('ep', 'fsdp')), may hold values from 0 to 3, all different within a row; in each aligned block of 128 rows (0 to 127, 128 to 255, ...) at most 128 rows name the same one
- chosen_logits: float32 [2048, 2], P(('ep', 'fsdp')), may hold values from -4 to 4
- routed_inputs: bfloat16 [4, 4, 4, 128, 4096], P('ep', None, 'fsdp'), may hold values from -6 to 6
- w_gate: bfloat16 [4, 4096, 512], P('ep', 'fsdp', 'tp'), may hold values from -0.09375 to 0.09375
- w_up: bfloat16 [4, 4096, 512], P('ep', 'fsdp', 'tp'), may hold values from -0.09375 to 0.09375
- w_down: bfloat16 [4, 512, 4096], P('ep', 'tp', 'fsdp'), may hold values from -0.25 to 0.25
Outputs:
- input_grad: bfloat16 [2048, 4096], P(('ep', 'fsdp'))
- logit_grad: float32 [2048, 2], P(('ep', 'fsdp'))
- grad_gate: float32 [4, 4096, 512], P('ep', 'fsdp', 'tp')
- grad_up: float32 [4, 4096, 512], P('ep', 'fsdp', 'tp')
- grad_down: float32 [4, 512, 4096], P('ep', 'tp', 'fsdp')
Inputs may be any that keep to these rules, and one draw needn't show every extreme that they name: Each row of routes names 2 different experts. In each token group of 128 consecutive rows no expert is named by more than 128 rows, a bound that some block reaches.
All inputs are finite; a program needn't handle non-finite values.
Results may differ from a plain program's by a relative error of at most 0.015.
Values may be sent and summed in bfloat16 or wider, within the bound.
A program may use at most 128 MiB of HBM per device.

v0:
```python
import jax
import jax.numpy as jnp
from jax import lax
from jax.sharding import PartitionSpec as P


def summed_rows(product, width, axis):
    whole = product(jnp.int32(0), width * lax.axis_size(axis)).astype(jnp.bfloat16)
    return lax.psum_scatter(whole, axis, scatter_dimension=0, tiled=True).astype(jnp.float32)


def slot_places(routes, experts, capacity):
    flat_routes = routes.reshape(-1)
    onehot = (flat_routes[:, None] == jnp.arange(experts, dtype=jnp.int32)[None, :]).astype(
        jnp.int32
    )
    earlier = (jnp.cumsum(onehot, axis=0) - onehot).astype(jnp.int32)
    position = jnp.sum(earlier * onehot, axis=1).astype(jnp.int32)
    return (flat_routes * capacity + position).astype(jnp.int32)


def weighted_rows(grad_rows, gate_probs):
    scaled = gate_probs[:, :, None] * grad_rows.astype(jnp.float32)[:, None, :]
    return scaled.astype(jnp.bfloat16).reshape(-1, grad_rows.shape[1])


def fill_slots(values, slot_index, total_slots):
    row_total = values.shape[0]
    source = jnp.full((total_slots,), row_total, jnp.int32)
    source = source.at[slot_index].set(jnp.arange(row_total, dtype=jnp.int32))
    padded = jnp.concatenate([values, jnp.zeros((1, values.shape[1]), values.dtype)], axis=0)
    return jnp.take(padded, source, axis=0)


def combine(returned, slot_index, tokens, per_token):
    picked = jnp.take(returned, slot_index, axis=0).astype(jnp.float32)
    return jnp.sum(picked.reshape(tokens, per_token, -1), axis=1).astype(jnp.bfloat16)


def transpose_dot(left, right):
    return lax.dot_general(
        left, right, (((0,), (0,)), ((), ())), preferred_element_type=jnp.float32
    )


def contract_last(left, right):
    return lax.dot_general(
        left, right, (((1,), (1,)), ((), ())), preferred_element_type=jnp.float32
    )


def body(out_grad, routes, chosen_logits, routed_inputs, w_gate, w_up, w_down):
    experts = lax.axis_size("ep")
    tp_count = lax.axis_size("tp")
    tokens, model_width = out_grad.shape
    per_token = routes.shape[1]
    capacity = routed_inputs.shape[3]
    gate_probs = jax.nn.softmax(chosen_logits, axis=-1)
    slot_index = slot_places(routes, experts, capacity)
    inputs = routed_inputs.reshape(-1, model_width)
    outgoing = fill_slots(weighted_rows(out_grad, gate_probs), slot_index, experts * capacity)
    arrived = lax.all_to_all(
        outgoing.reshape(experts, capacity, model_width),
        "ep",
        split_axis=0,
        concat_axis=0,
        tiled=True,
    )
    scaled = arrived.reshape(-1, model_width)
    gate_full, up_full, down_full = (
        lax.all_gather(w_gate, "fsdp", axis=1, tiled=True),
        lax.all_gather(w_up, "fsdp", axis=1, tiled=True),
        lax.all_gather(w_down, "fsdp", axis=2, tiled=True),
    )
    gate_full = gate_full[0]
    up_full = up_full[0]
    down_full = down_full[0]
    gate_act = jnp.dot(inputs, gate_full, preferred_element_type=jnp.float32)
    up_act = jnp.dot(inputs, up_full, preferred_element_type=jnp.float32)
    sigmoid_gate = jax.nn.sigmoid(gate_act)
    silu_gate = gate_act * sigmoid_gate
    hidden = (silu_gate * up_act).astype(jnp.bfloat16)
    hidden_grad = contract_last(scaled, down_full)
    products = jnp.sum(hidden_grad * hidden.astype(jnp.float32), axis=1)
    up_grad = (hidden_grad * silu_gate).astype(jnp.bfloat16)
    gate_grad = (
        hidden_grad * up_act * sigmoid_gate * (1.0 + gate_act * (1.0 - sigmoid_gate))
    ).astype(jnp.bfloat16)
    slot_part = contract_last(gate_grad, gate_full) + contract_last(up_grad, up_full)
    pair_grads = jnp.concatenate([gate_grad, up_grad], axis=1)

    def grad_term(first_row, row_count):
        input_cols = lax.dynamic_slice_in_dim(inputs, first_row, row_count, 1)
        scaled_cols = lax.dynamic_slice_in_dim(scaled, first_row, row_count, 1)
        gate_up_part = transpose_dot(input_cols, pair_grads)
        down_part = transpose_dot(scaled_cols, hidden)
        return jnp.concatenate([gate_up_part, down_part], axis=1)

    grad_rows = summed_rows(grad_term, model_width // lax.axis_size("fsdp"), "fsdp")
    hidden_units = hidden.shape[1]
    grad_gate = grad_rows[:, :hidden_units][None]
    grad_up = grad_rows[:, hidden_units : 2 * hidden_units][None]
    grad_down = grad_rows[:, 2 * hidden_units :].T[None]
    narrow = model_width // tp_count
    column_sum = lax.psum_scatter(
        slot_part.astype(jnp.bfloat16), "tp", scatter_dimension=1, tiled=True
    ).astype(jnp.float32)
    product_sum = lax.psum(products.astype(jnp.bfloat16), "tp").astype(jnp.float32)
    leaving = (
        column_sum.astype(jnp.bfloat16).reshape(experts, capacity, narrow),
        product_sum.astype(jnp.bfloat16).reshape(experts, capacity),
    )
    back_rows, back_products = (
        lax.all_to_all(leaving[0], "ep", split_axis=0, concat_axis=0, tiled=True),
        lax.all_to_all(leaving[1], "ep", split_axis=0, concat_axis=0, tiled=True),
    )
    combined = combine(back_rows.reshape(-1, narrow), slot_index, tokens, per_token)
    input_grad = lax.all_gather(combined, "tp", axis=1, tiled=True)
    chosen = (
        jnp.take(back_products.reshape(-1), slot_index)
        .astype(jnp.float32)
        .reshape(tokens, per_token)
    )
    logit_grad = chosen - gate_probs * jnp.sum(chosen, axis=1, keepdims=True)
    return (input_grad, logit_grad, grad_gate, grad_up, grad_down)


def solution(mesh):
    in_specs = (
        P(("ep", "fsdp"), None),
        P(("ep", "fsdp"), None),
        P(("ep", "fsdp"), None),
        P("ep", None, "fsdp", None, None),
        P("ep", "fsdp", "tp"),
        P("ep", "fsdp", "tp"),
        P("ep", "tp", "fsdp"),
    )
    out_specs = (
        P(("ep", "fsdp"), None),
        P(("ep", "fsdp"), None),
        P("ep", "fsdp", "tp"),
        P("ep", "fsdp", "tp"),
        P("ep", "tp", "fsdp"),
    )
    return jax.shard_map(body, mesh=mesh, in_specs=in_specs, out_specs=out_specs, check_vma=False)
```

profile of v0, /device:TPU:0, one launch (start us, length us, event | category | flops | bytes accessed | tf_op | source)
XLA Modules:
  0.0 294.9 jit_solution(5243169975518760738)
XLA Ops:
  7.2 0.7 all-gather.9.cloned.1.call-update
  7.9 0.7 all-gather.7.cloned.1.call-update
  8.6 0.8 copy.38
  9.7 0.7 broadcast_multiply_fusion
  10.4 1.2 reduce-window.6
  12.3 1.4 scatter_custom_fusion
  13.8 0.7 reduce_max.9
  14.4 0.7 fusion.21
  15.1 0.7 fusion.20
  16.1 5.3 %mul.79 = f32[128,2,4096]{2,1,0:T(2,128)} broadcast(bf16[128,4096]{1,0:T(8,128)(2,1)} %param.7), dimensions={0,2} | broadcast | bytes 5242880 | tf_op jit(solution)/shard_map/mul | solution.py:23
  21.4 6.0 %mul.80 = f32[256,4096]{1,0:T(8,128)} reshape(f32[128,2,4096]{2,1,0:T(2,128)} %mul.79) | data formatting | bytes 8388608 | tf_op jit(solution)/shard_map/mul | solution.py:23
  27.4 2.6 multiply_convert_fusion
  30.1 0.3 concatenate.10
  30.3 4.4 %gather_fusion = bf16[512,4096]{1,0:T(8,128)(2,1)} fusion(bf16[257,4096]{1,0:T(8,128)(2,1)S(1)} %concatenate.10, s32[1024]{0:T(1024)S(1)} %pad_clamp_fusion.1), kind=kCustom, calls=%fused_computation | custom fusion | bytes 8390656 | tf_op jit(solution)/shard_map/jit(_take)/gather | solution.py:32
  34.7 4.6 %broadcast_select_fusion = bf16[4,128,4096]{2,1,0:T(8,128)(2,1)} fusion(bf16[4,128,4096]{2,1,0:T(8,128)(2,1)} %bitcast.67, pred[4,128]{1,0:T(4,128)(4,1)S(1)} %and_bitcast_fusion), kind=kLoop, calls=%fused_computation.10 | loop fusion | flops 2097152 | bytes 8389120 | tf_op jit(solution)/shard_map/jit(_take)/select_n | solution.py:32
  39.3 6.4 %all-to-all-start = ((bf16[4,128,4096]{2,1,0:T(8,128)(2,1)}), bf16[4,128,4096]{2,1,0:T(8,128)(2,1)}, u32[]{:S(2)}, u32[]{:S(2)}) async-start(bf16[4,128,4096]{2,1,0:T(8,128)(2,1)} %broadcast_select_fusion), calls=%async_computation | async-start | bytes 8388608 | tf_op jit(solution)/shard_map/all_to_all | solution.py:62
  45.7 0.7 all-gather.5.cloned.1.call-update
  46.4 0.2 reduce-scatter.3.cloned.1.call-start
  46.6 4.2 %fusion.3 = f32[512,256]{0,1:T(8,128)S(1)} fusion(bf16[512,4096]{1,0:T(8,128)(2,1)} %bitcast.74, bf16[1,4096,256]{2,1,0:T(8,128)(2,1)} %all-gather.9.cloned.1.call-done), kind=kOutput, calls=%fused_computation.13 | convolution fusion | flops 1073741824 | bytes 6815744 | tf_op jit(solution)/shard_map/dot_general | solution.py:78
  50.8 8.0 %all-gather.7.cloned.1.call-done = bf16[1,4096,256]{2,1,0:T(8,128)(2,1)} async-done(((bf16[1,1024,256]{2,1,0:T(8,128)(2,1)}), bf16[1,4096,256]{2,1,0:T(8,128)(2,1)}) %all-gather.7.cloned.1.call-update) | async-done | bytes 2097168 | tf_op jit(solution)/shard_map/all_gather | solution.py:72
  58.8 4.2 %fusion.6 = f32[512,256]{0,1:T(8,128)S(1)} fusion(bf16[512,4096]{1,0:T(8,128)(2,1)} %bitcast.75, bf16[1,4096,256]{2,1,0:T(8,128)(2,1)} %all-gather.7.cloned.1.call-done), kind=kOutput, calls=%fused_computation.16 | convolution fusion | flops 1073741824 | bytes 6815744 | tf_op jit(solution)/shard_map/dot_general | solution.py:79
  63.0 19.9 %all-gather.5.cloned.1.call-done = bf16[1,256,4096]{2,1,0:T(8,128)(2,1)} async-done(((bf16[1,256,1024]{2,1,0:T(8,128)(2,1)}), bf16[1,256,4096]{2,1,0:T(8,128)(2,1)}) %all-gather.5.cloned.1.call-update) | async-done | bytes 2097168 | tf_op jit(solution)/shard_map/all_gather | solution.py:73
  82.9 56.1 %all-to-all-done = bf16[4,128,4096]{2,1,0:T(8,128)(2,1)} async-done(((bf16[4,128,4096]{2,1,0:T(8,128)(2,1)}), bf16[4,128,4096]{2,1,0:T(8,128)(2,1)}, u32[]{:S(2)}, u32[]{:S(2)}) %all-to-all-start) | async-done | bytes 4194336 | tf_op jit(solution)/shard_map/all_to_all | solution.py:62
  139.0 4.5 %multiply_reduce_fusion = (bf16[512]{0:T(512)(128)(2,1)S(1)}, bf16[512,256]{0,1:T(8,128)(2,1)S(1)}, bf16[512,256]{0,1:T(8,128)(2,1)S(1)}, bf16[512,256]{0,1:T(8,128)(2,1)S(1)}) fusion(f32[512,256]{0,1:T(8,128)S(1)} %fusion.6, f32[512,256]{0,1:T(8,128)S(1)} %fusion.3, bf16[512,4096]{1,0:T(8,128)(2,1)} %bitcast.6, ...), kind=kOutput, calls=%fused_computation.28 | convolution fusion | flops 1076100608 | bytes 8127488 | tf_op jit(solution)/shard_map/dot_general | solution.py:47
  143.5 1.3 fusion.1
  144.8 0.3 copy-done
  145.1 3.4 %add_convert_fusion = bf16[512,4096]{1,0:T(8,128)(2,1)} fusion(f32[512,4096]{1,0:T(8,128)S(1)} %fusion.1, bf16[512,256]{0,1:T(8,128)(2,1)S(1)} %get-tuple-element.33, bf16[1,4096,256]{2,1,0:T(8,128)(2,1)S(1)} %copy-done), kind=kOutput, calls=%fused_computation.4 | convolution fusion | flops 1077936128 | bytes 14942208 | tf_op jit(solution)/shard_map/dot_general | solution.py:47
  148.6 3.7 %convolution_convert_fusion.1 = bf16[4096,256]{0,1:T(8,128)(2,1)S(1)} fusion(bf16[512,256]{0,1:T(8,128)(2,1)S(1)} %get-tuple-element.28, bf16[512,4096]{1,0:T(8,128)(2,1)} %bitcast.6), kind=kOutput, calls=%fused_computation.8 | convolution fusion | flops 1074790400 | bytes 6553600 | tf_op jit(solution)/shard_map/dot_general | solution.py:41
  152.3 2.4 fusion
  154.7 3.4 %pad_maximum_fusion = bf16[4096,768]{0,1:T(8,128)(2,1)} fusion(bf16[4096,256]{0,1:T(8,128)(2,1)S(1)} %convolution_convert_fusion.1, bf16[4096,512]{0,1:T(8,128)(2,1)S(1)} %fusion), kind=kLoop, calls=%fused_computation.5 | loop fusion | flops 12582912 | bytes 12582912 | tf_op jit(solution)/shard_map/concatenate | solution.py:97
  158.1 5.0 %psum.7 = bf16[4,1,128]{2,0,1:T(4,128)(2,1)S(1)} all-reduce(bf16[4,1,128]{2,0,1:T(4,128)(2,1)S(1)} %bitcast.73), channel_id=1, replica_groups=mesh['ep'=4,'fsdp'=4,'tp'=2] {'tp'}, use_global_device_ids=true, to_apply=%region_9.10 | all-reduce | flops 512 | bytes 2048 | tf_op jit(solution)/shard_map/psum | solution.py:108
  163.2 8.2 %all_to_all.19 = bf16[4,1,128]{2,1,0:T(2,128)(2,1)S(1)} all-to-all(bf16[4,1,128]{2,1,0:T(2,128)(2,1)S(1)} %copy.46), channel_id=1, replica_groups=mesh['ep'=4,'fsdp'=4,'tp'=2] {'ep'}, dimensions={0} | all-to-all | bytes 2048 | tf_op jit(solution)/shard_map/all_to_all | solution.py:115
  171.4 31.0 %reduce-scatter.3.cloned.1.call-done = bf16[512,2048]{1,0:T(8,128)(2,1)} async-done(((bf16[512,4096]{1,0:T(8,128)(2,1)}), bf16[512,2048]{1,0:T(8,128)(2,1)}) %reduce-scatter.3.cloned.1.call-update) | async-done | bytes 2097168 | tf_op jit(solution)/shard_map/reduce_scatter | solution.py:105
  202.4 4.6 %all-to-all-start.1 = ((bf16[4,128,2048]{2,1,0:T(8,128)(2,1)}), bf16[4,128,2048]{2,1,0:T(8,128)(2,1)S(1)}, u32[]{:S(2)}, u32[]{:S(2)}) async-start(bf16[4,128,2048]{2,1,0:T(8,128)(2,1)} %bitcast.68), calls=%async_computation.2 | async-start | bytes 4194304 | tf_op jit(solution)/shard_map/all_to_all | solution.py:114
  207.2 1.9 gather_fusion.2
  209.2 0.2 gather.23
  209.6 45.3 %all-to-all-done.1 = bf16[4,128,2048]{2,1,0:T(8,128)(2,1)S(1)} async-done(((bf16[4,128,2048]{2,1,0:T(8,128)(2,1)}), bf16[4,128,2048]{2,1,0:T(8,128)(2,1)S(1)}, u32[]{:S(2)}, u32[]{:S(2)}) %all-to-all-start.1) | async-done | bytes 2097184 | tf_op jit(solution)/shard_map/all_to_all | solution.py:114
  254.9 1.4 gather_fusion.1
  256.3 0.7 gather.21
  257.0 3.2 %fusion.10 = bf16[128,2048]{1,0:T(8,128)(2,1)} fusion(bf16[128,2,2048]{2,1,0:T(2,128)(2,1)S(1)} %gather.21, pred[128,2]{1,0:T(8,128)(4,1)S(1)} %copy.43), kind=kLoop, calls=%fused_computation.21 | loop fusion | flops 786432 | bytes 1573120 | tf_op jit(solution)/shard_map/reduce_sum | solution.py:37
  260.2 0.6 convert_subtract_fusion
  260.8 1.8 reduce-scatter.5.cloned.1.call-done
  262.6 1.8 convert_element_type.58
  264.4 1.2 slice_bitcast_fusion
  265.6 1.3 copy.48
  266.9 1.3 copy.49
  268.2 17.6 %all-gather.11.cloned.1.call-done = bf16[128,4096]{1,0:T(8,128)(2,1)} async-done(((bf16[128,2048]{1,0:T(8,128)(2,1)}), bf16[128,4096]{1,0:T(8,128)(2,1)}) %all-gather.11.cloned.1.call-update) | async-done | bytes 1048592 | tf_op jit(solution)/shard_map/all_gather | solution.py:118
  285.8 2.3 copy.53
  (45 shorter events, 1.9 us)
Async XLA Ops:
  7.2 39.5 %all-gather.9.cloned.1.call-start = ((), (), s32[]{:S(2)}) async-start(), calls=%async_computation.7 | async-start | bytes 2621440 | tf_op jit(solution)/shard_map/all_gather | solution.py:71
  7.9 50.9 %all-gather.7.cloned.1.call-start = ((), (), s32[]{:S(2)}) async-start(), calls=%async_computation.6 | async-start | bytes 2621440 | tf_op jit(solution)/shard_map/all_gather | solution.py:72
  39.3 99.7 %all-to-all-start = ((bf16[4,128,4096]{2,1,0:T(8,128)(2,1)}), bf16[4,128,4096]{2,1,0:T(8,128)(2,1)}, u32[]{:S(2)}, u32[]{:S(2)}) async-start(bf16[4,128,4096]{2,1,0:T(8,128)(2,1)} %broadcast_select_fusion), calls=%async_computation | async-start | bytes 8388608 | tf_op jit(solution)/shard_map/all_to_all | solution.py:62
  45.7 37.2 %all-gather.5.cloned.1.call-start = ((), (), s32[]{:S(2)}) async-start(), calls=%async_computation.5 | async-start | bytes 2621440 | tf_op jit(solution)/shard_map/all_gather | solution.py:73
  46.4 156.0 %reduce-scatter.3.cloned.1.call-start = ((), (), s32[]{:S(2)}) async-start(), calls=%async_computation.8 | async-start | bytes 6291456 | tf_op jit(solution)/shard_map/reduce_scatter | solution.py:105
  139.0 4.5 %copy-start.1 = (bf16[1,4096,256]{2,1,0:T(8,128)(2,1)S(1)}, bf16[1,4096,256]{2,1,0:T(8,128)(2,1)}, u32[]{:S(2)}) copy-start(bf16[1,4096,256]{2,1,0:T(8,128)(2,1)} %all-gather.9.cloned.1.call-done) | copy-start | bytes 6291460
  143.5 1.6 copy-start
  148.5 114.0 %reduce-scatter.5.cloned.1.call-start = ((), (), s32[]{:S(2)}) async-start(), calls=%async_computation.10 | async-start | bytes 7864320 | tf_op jit(solution)/shard_map/reduce_scatter | solution.py:9
  148.6 3.7 %copy-start.4 = (bf16[1,4,1,128,4096]{4,3,2,1,0:T(8,128)(2,1)S(1)}, bf16[1,4,1,128,4096]{4,3,2,1,0:T(8,128)(2,1)}, u32[]{:S(2)}) copy-start(bf16[1,4,1,128,4096]{4,3,2,1,0:T(8,128)(2,1)} %param.10) | copy-start | bytes 12582916
  158.1 51.3 %copy-start.3 = (s32[128,2]{0,1:T(2,128)S(1)}, s32[128,2]{0,1:T(2,128)}, u32[]{:S(2)}) copy-start(s32[128,2]{0,1:T(2,128)} %param.8) | copy-start | bytes 3076
  202.4 52.5 %all-to-all-start.1 = ((bf16[4,128,2048]{2,1,0:T(8,128)(2,1)}), bf16[4,128,2048]{2,1,0:T(8,128)(2,1)S(1)}, u32[]{:S(2)}, u32[]{:S(2)}) async-start(bf16[4,128,2048]{2,1,0:T(8,128)(2,1)} %bitcast.68), calls=%async_computation.2 | async-start | bytes 4194304 | tf_op jit(solution)/shard_map/all_to_all | solution.py:114
  207.0 78.8 %all-gather.11.cloned.1.call-start = ((), (), s32[]{:S(2)}) async-start(), calls=%async_computation.9 | async-start | bytes 1572864 | tf_op jit(solution)/shard_map/all_gather | solution.py:118
  256.3 3.9 %copy-start.2 = (f32[128,2]{0,1:T(2,128)S(1)}, f32[128,2]{0,1:T(2,128)}, u32[]{:S(2)}) copy-start(f32[128,2]{0,1:T(2,128)} %param.9) | copy-start | bytes 3076
Sparse Core Ops, SparseCore 0:
  9.5 25.1 all-gather.8
  36.3 22.4 all-gather.6
  60.4 22.4 all-gather.4
  148.7 53.6 reduce-scatter.2
  204.8 57.7 reduce-scatter.4
  264.5 21.1 all-gather.10
where the time goes:
time: 296 us; the launch traced here: 295 us
  waiting for transfers between devices  182 us (61%)
  local copies, waits for them, and re-layouts  30.1 us (10%)
  matrix products  23.6 us (8%)
  other arithmetic  20.4 us (7%)
  between operations  14.3 us (5%)
  blocking collectives  13.2 us (4%)
  starting transfers between devices  11.3 us (4%)
    all_to_all x1, waiting for transfers between devices, body(): lax.all_to_all(outgoing.reshape(experts, capacity, model_width), 'ep', sp...  56.1 us
    all_to_all x1, waiting for transfers between devices, body(): lax.all_to_all(leaving[0], 'ep', split_axis=0, concat_axis=0, tiled=True)  45.3 us
    reduce_scatter x1, waiting for transfers between devices, body(): lax.psum_scatter(slot_part.astype(jnp.bfloat16), 'tp', scatter_dimension=...  31 us
    all_gather x1, waiting for transfers between devices, body(): lax.all_gather(w_down, 'fsdp', axis=2, tiled=True)  19.9 us
    all_gather x1, waiting for transfers between devices, body(): input_grad = lax.all_gather(combined, 'tp', axis=1, tiled=True)  17.6 us
    mul x3, local copies, waits for them, and re-layouts, weighted_rows(): scaled = gate_probs[:, :, None] * grad_rows.astype(jnp.float32)[:, None, :]  11.5 us
    dot_general x3, matrix products, contract_last(): lax.dot_general(left, right, (((1,), (1,)), ((), ())), preferred_element_...  9.23 us
    all_to_all x1, blocking collectives, body(): lax.all_to_all(leaving[1], 'ep', split_axis=0, concat_axis=0, tiled=True)  8.2 us
  transfers between devices with their start and end apart: 8, of which 7 were waited for; matrix products, arithmetic and copies ran while one was open for 21% of the time, Pallas kernels for 0%

commit v1 on v0

v1 whole, which is shorter than its diff:
```python
import functools

import jax
import jax.numpy as jnp
from jax import lax
from jax.experimental import pallas as pl
from jax.experimental.pallas import tpu as pltpu
from jax.sharding import PartitionSpec as P

MESH = pl.DeviceIdType.MESH
AXES = ("ep", "fsdp", "tp")


def when(cond, fn):
    pl.when(cond)(fn)


def entry_barrier():
    barrier = pltpu.get_barrier_semaphore()
    for axis in AXES:
        size, me = lax.axis_size(axis), lax.axis_index(axis)
        for step in range(1, size):
            if step not in (1, size - 1) and axis != "tp":
                continue
            peer = lax.rem(me + step, size)
            pl.semaphore_signal(barrier, inc=1, device_id={axis: peer}, device_id_type=MESH)
    count = 0
    for axis in AXES:
        size = lax.axis_size(axis)
        count += size - 1 if axis == "tp" else min(2, size - 1)
    pl.semaphore_wait(barrier, count)


def gather_kernel(
    rows_ref, meta_ref, gate_ref, up_ref, down_ref,
    rows_out, meta_out, gate_out, up_out, down_out,
    send_sem, recv_sem, fsend_sem, frecv_sem, tsend_sem, trecv_sem,
):
    ep, fs, tp = (lax.axis_index(a) for a in AXES)
    n_ep, n_fs, n_tp = (lax.axis_size(a) for a in AXES)
    width = rows_ref.shape[1] // n_tp
    depth = down_ref.shape[1]

    def cols(k):
        return pl.ds(pl.multiple_of(k * width, width), width)

    def chunk(k):
        return pl.ds(pl.multiple_of(k * depth, depth), depth)

    ep_streams = (
        (rows_ref.at[:, cols(tp)], lambda b: rows_out.at[b, :, cols(tp)]),
        (meta_ref, lambda b: meta_out.at[b]),
    )
    fs_streams = (
        (gate_ref, lambda b: gate_out.at[b]),
        (up_ref, lambda b: up_out.at[b]),
        (down_ref, lambda b: down_out.at[:, chunk(b)]),
    )

    def copy(axis, index, stream, block, own, way, peer):
        source, place = stream
        sends, recvs = (send_sem, recv_sem) if axis == "ep" else (fsend_sem, frecv_sem)
        return pltpu.make_async_remote_copy(
            src_ref=source if own else place(block),
            dst_ref=place(block),
            send_sem=sends.at[index, way, block],
            recv_sem=recvs.at[index, block],
            device_id={axis: peer},
            device_id_type=MESH,
        )

    def tp_copy(block, step, owner, peer):
        return pltpu.make_async_remote_copy(
            src_ref=rows_out.at[block, :, cols(owner)],
            dst_ref=rows_out.at[block, :, cols(owner)],
            send_sem=tsend_sem.at[block, step],
            recv_sem=trecv_sem.at[block, step],
            device_id={"tp": peer},
            device_id_type=MESH,
        )

    entry_barrier()

    def advance(axis, me, size, streams, r, finish):
        for way, sign in ((0, 1), (1, -1)):
            block = me - sign * r
            have = jnp.logical_and(block >= 0, block < size)
            peer = me + sign
            more = jnp.logical_and(peer >= 0, peer < size)
            for index, stream in enumerate(streams):
                if not finish and r > 0:
                    def arrived(index=index, stream=stream):
                        copy(axis, index, stream, block, False, way, me - sign).wait_recv()
                        if axis == "ep" and index == 0:
                            for step in range(1, n_tp):
                                tp_copy(block, step - 1, tp, lax.rem(tp + step, n_tp)).start()
                    when(have, arrived)

                if r < size - 1:
                    def send(index=index, stream=stream):
                        c = copy(axis, index, stream, block, r == 0, way, peer)
                        if finish:
                            c.wait_send()
                        else:
                            c.start()
                    when(jnp.logical_and(have, more), send)

    for finish in (False, True):
        for r in range(max(n_ep, n_fs)):
            if r < n_ep:
                advance("ep", ep, n_ep, ep_streams, r, finish)
            if r < n_fs:
                advance("fsdp", fs, n_fs, fs_streams, r, finish)
            if r == 0 and not finish:
                rows_out[ep] = rows_ref[...]
                meta_out[ep] = meta_ref[...]
                gate_out[fs] = gate_ref[...]
                up_out[fs] = up_ref[...]
                down_out[:, chunk(fs)] = down_ref[...]
    for block in range(n_ep):
        def close(block=block):
            for step in range(1, n_tp):
                tp_copy(block, step - 1, tp, lax.rem(tp + step, n_tp)).wait_send()
                owner = lax.rem(tp + n_tp - step, n_tp)
                tp_copy(block, step - 1, owner, owner).wait_recv()
        when(block != ep, close)


def gather_all(rows, meta, gate, up, down):
    n_ep, n_fs, n_tp = (lax.axis_size(a) for a in AXES)
    vmem = pl.BlockSpec(memory_space=pltpu.VMEM)
    dma = pltpu.SemaphoreType.DMA
    return pl.pallas_call(
        gather_kernel,
        out_shape=(
            jax.ShapeDtypeStruct((n_ep, *rows.shape), rows.dtype),
            jax.ShapeDtypeStruct((n_ep, *meta.shape), meta.dtype),
            jax.ShapeDtypeStruct((n_fs, *gate.shape), gate.dtype),
            jax.ShapeDtypeStruct((n_fs, *up.shape), up.dtype),
            jax.ShapeDtypeStruct((down.shape[0], n_fs * down.shape[1]), down.dtype),
        ),
        in_specs=[vmem] * 5,
        out_specs=[vmem] * 5,
        scratch_shapes=[
            dma((2, 2, n_ep)),
            dma((2, n_ep)),
            dma((3, 2, n_fs)),
            dma((3, n_fs)),
            dma((n_ep, max(1, n_tp - 1))),
            dma((n_ep, max(1, n_tp - 1))),
        ],
        compiler_params=pltpu.CompilerParams(
            collective_id=0, has_side_effects=True, vmem_limit_bytes=48 * 1024 * 1024
        ),
    )(rows, meta, gate, up, down)


def transpose_dot(left, right):
    return lax.dot_general(
        left, right, (((0,), (0,)), ((), ())), preferred_element_type=jnp.float32
    )


def contract_last(left, right):
    return lax.dot_general(
        left, right, (((1,), (1,)), ((), ())), preferred_element_type=jnp.float32
    )


def body(out_grad, routes, chosen_logits, routed_inputs, w_gate, w_up, w_down):
    groups = lax.axis_size("ep")
    me = lax.axis_index("ep")
    tokens, model_width = out_grad.shape
    per_token = routes.shape[1]
    capacity = routed_inputs.shape[3]
    inputs = routed_inputs.reshape(-1, model_width)
    own_probs = jax.nn.softmax(chosen_logits, axis=-1)
    meta = jnp.concatenate(
        [
            routes.astype(jnp.float32).T,
            own_probs.T,
            jnp.zeros((8 - 2 * per_token, tokens), jnp.float32),
        ],
        axis=0,
    )
    rows, meta_all, gate_full, up_full, down_full = gather_all(
        out_grad, meta, w_gate[0], w_up[0], w_down[0]
    )
    gate_full = gate_full.reshape(model_width, -1)
    up_full = up_full.reshape(model_width, -1)
    chosen_here = (meta_all[:, :per_token] == me.astype(jnp.float32)).astype(jnp.float32)
    weight = jnp.sum(chosen_here * meta_all[:, per_token : 2 * per_token], axis=1)
    mask = jnp.sum(chosen_here, axis=1)
    order = jnp.arange(tokens)
    earlier = (order[:, None] < order[None, :]).astype(jnp.bfloat16)
    place = jnp.dot(mask.astype(jnp.bfloat16), earlier, preferred_element_type=jnp.float32)
    hit = (place[:, None, :] == jnp.arange(capacity, dtype=jnp.float32)[None, :, None]) & (
        mask[:, None, :] > 0
    )
    select = hit.astype(jnp.bfloat16)
    slot_weight = jnp.sum(jnp.where(hit, weight[:, None, :], 0.0), axis=2)
    picked = lax.dot_general(
        select, rows, (((2,), (1,)), ((0,), (0,))), preferred_element_type=jnp.float32
    )
    scaled = (picked * slot_weight[:, :, None]).astype(jnp.bfloat16).reshape(-1, model_width)

    gate_act = jnp.dot(inputs, gate_full, preferred_element_type=jnp.float32)
    up_act = jnp.dot(inputs, up_full, preferred_element_type=jnp.float32)
    sigmoid_gate = jax.nn.sigmoid(gate_act)
    silu_gate = gate_act * sigmoid_gate
    hidden = (silu_gate * up_act).astype(jnp.bfloat16)
    hidden_grad = contract_last(scaled, down_full)
    products = jnp.sum(hidden_grad * hidden.astype(jnp.float32), axis=1)
    up_grad = (hidden_grad * silu_gate).astype(jnp.bfloat16)
    gate_grad = (
        hidden_grad * up_act * sigmoid_gate * (1.0 + gate_act * (1.0 - sigmoid_gate))
    ).astype(jnp.bfloat16)
    pair_grads = jnp.concatenate([gate_grad, up_grad], axis=1)
    hidden_units = hidden.shape[1]
    pair_rows = lax.dot_general(
        select,
        pair_grads.reshape(groups, capacity, -1),
        (((1,), (1,)), ((0,), (0,))),
        preferred_element_type=jnp.float32,
    ).astype(jnp.bfloat16).reshape(groups * tokens, -1)
    token_part = contract_last(pair_rows[:, :hidden_units], gate_full) + contract_last(
        pair_rows[:, hidden_units:], up_full
    )
    column_sum = lax.psum_scatter(
        token_part.astype(jnp.bfloat16), "tp", scatter_dimension=1, tiled=True
    )
    combined = lax.psum_scatter(column_sum, "ep", scatter_dimension=0, tiled=True)
    input_grad = lax.all_gather(combined, "tp", axis=1, tiled=True)

    token_products = jnp.sum(
        jnp.where(hit, products.reshape(groups, capacity)[:, :, None], 0.0), axis=1
    )
    pair_products = chosen_here * token_products[:, None, :]
    product_sum = lax.psum(pair_products, ("ep", "tp"))
    chosen = lax.dynamic_index_in_dim(product_sum, me, 0, keepdims=False).T
    chosen = lax.reduce_precision(chosen, 8, 7)
    logit_grad = chosen - own_probs * jnp.sum(chosen, axis=1, keepdims=True)

    gate_up = transpose_dot(inputs, pair_grads)
    down_part = transpose_dot(scaled, hidden)
    whole = jnp.concatenate([gate_up, down_part], axis=1).astype(jnp.bfloat16)
    grad_rows = lax.psum_scatter(whole, "fsdp", scatter_dimension=0, tiled=True).astype(
        jnp.float32
    )
    grad_gate = grad_rows[:, :hidden_units][None]
    grad_up = grad_rows[:, hidden_units : 2 * hidden_units][None]
    grad_down = grad_rows[:, 2 * hidden_units :].T[None]
    return (input_grad, logit_grad, grad_gate, grad_up, grad_down)


def solution(mesh):
    in_specs = (
        P(("ep", "fsdp"), None),
        P(("ep", "fsdp"), None),
        P(("ep", "fsdp"), None),
        P("ep", None, "fsdp", None, None),
        P("ep", "fsdp", "tp"),
        P("ep", "fsdp", "tp"),
        P("ep", "tp", "fsdp"),
    )
    out_specs = (
        P(("ep", "fsdp"), None),
        P(("ep", "fsdp"), None),
        P("ep", "fsdp", "tp"),
        P("ep", "fsdp", "tp"),
        P("ep", "tp", "fsdp"),
    )
    return jax.shard_map(body, mesh=mesh, in_specs=in_specs, out_specs=out_specs, check_vma=False)
```

time: 296 us -> 280 us (0.946)
  Pallas kernels: 0 us -> 60.3 us
  waiting for transfers between devices: 182 us -> 143 us
  local copies, waits for them, and re-layouts: 30.1 us -> 12.4 us
  other arithmetic: 20.4 us -> 9.27 us
  starting transfers between devices: 11.3 us -> 0.34 us
  blocking collectives: 13.2 us -> 19.4 us
  matrix products: 23.6 us -> 20.5 us
    all_to_all x2 -> x0, waiting for transfers between devices: 101 us -> none  [the longest x1 56.1 us: body(): lax.all_to_all(outgoing.reshape(experts, capacity, model_width), 'ep', sp...]
    reduce_scatter x2 -> x3, waiting for transfers between devices: 32.8 us -> 126 us  [the longest x1 50.6 us: body(): lax.psum_scatter(token_part.astype(jnp.bfloat16), 'tp', scatter_dimension...]
    pallas_call x0 -> x1, Pallas kernels: none -> 60.3 us  [gather_all(): pl.pallas_call(gather_kernel, out_shape=(jax.ShapeDtypeStruct((n_ep, *row...]
    all_gather x3 -> x0, waiting for transfers between devices: 27.9 us -> none  [the longest x1 19.9 us: body(): lax.all_gather(w_down, 'fsdp', axis=2, tiled=True)]
    psum x1, blocking collectives: 5.02 us -> 19.4 us  [body(): product_sum = lax.psum(pair_products, ('ep', 'tp'))]
    mul x5 -> x0, local copies, waits for them, and re-layouts: 11.7 us -> none  [the longest x3 11.5 us: weighted_rows(): scaled = gate_probs[:, :, None] * grad_rows.astype(jnp.float32)[:, None, :]]
    all_to_all x2 -> x0, starting transfers between devices: 11 us -> none  [the longest x1 6.38 us: body(): lax.all_to_all(outgoing.reshape(experts, capacity, model_width), 'ep', sp...]
    gather x6 -> x0, local copies, waits for them, and re-layouts: 8.59 us -> none  [the longest x1 4.35 us: fill_slots(): return jnp.take(padded, source, axis=0)]
  transfers between devices with their start and end apart: 8 -> 4, of which waited for: 7 -> 4; matrix products, arithmetic and copies ran while one was open for 21% -> 6% of each run, Pallas kernels for 0% -> 0%
where the time goes in v1:
time: 280 us; the launch traced here: 279 us
  waiting for transfers between devices  143 us (51%)
  Pallas kernels  60.3 us (22%)
  matrix products  20.5 us (7%)
  blocking collectives  19.4 us (7%)
  between operations  14 us (5%)
  local copies, waits for them, and re-layouts  12.4 us (4%)
  other arithmetic  9.27 us (3%)
    pallas_call x1, Pallas kernels, gather_all(): pl.pallas_call(gather_kernel, out_shape=(jax.ShapeDtypeStruct((n_ep, *row...  60.3 us
    reduce_scatter x1, waiting for transfers between devices, body(): lax.psum_scatter(token_part.astype(jnp.bfloat16), 'tp', scatter_dimension...  50.6 us
    reduce_scatter x1, waiting for transfers between devices, body(): lax.psum_scatter(whole, 'fsdp', scatter_dimension=0, tiled=True)  38.9 us
    reduce_scatter x1, waiting for transfers between devices, body(): lax.psum_scatter(column_sum, 'ep', scatter_dimension=0, tiled=True)  36.5 us
    psum x1, blocking collectives, body(): product_sum = lax.psum(pair_products, ('ep', 'tp'))  19.4 us
    all_gather x1, waiting for transfers between devices, body(): input_grad = lax.all_gather(combined, 'tp', axis=1, tiled=True)  17 us
    unnamed x31, local copies, waits for them, and re-layouts  11 us
    dot_general x3, matrix products, contract_last(): lax.dot_general(left, right, (((1,), (1,)), ((), ())), preferred_element_...  7.07 us
  transfers between devices with their start and end apart: 4, of which 4 were waited for; matrix products, arithmetic and copies ran while one was open for 6% of the time, Pallas kernels for 0%

profile of v1, /device:TPU:0, one launch (start us, length us, event | category | flops | bytes accessed | tf_op | source)
XLA Modules:
  0.0 279.3 jit_solution(1655051413195634840)
XLA Ops:
  7.2 0.0 reduce-scatter.4.cloned.1.call-start
  7.2 0.7 reduce_max.9
  7.9 0.7 fusion.15
  8.6 0.7 fusion.30
  9.3 0.7 convert_bitcast_fusion
  10.0 1.2 copy-done
  11.2 1.0 copy-done.1
  12.3 1.0 copy-done.2
  13.3 1.0 copy-done.3
  14.4 60.3 %shard_map.110 = (bf16[4,128,4096]{2,1,0:T(8,128)(2,1)}, f32[4,8,128]{2,1,0:T(8,128)S(1)}, bf16[4,1024,256]{2,1,0:T(8,128)(2,1)S(1)}, bf16[4,1024,256]{2,1,0:T(8,128)(2,1)}, bf16[256,4096]{1,0:T(8,128)(2,1)}) custom-call(bf16[128,4096]{1,0:T(8,128)(2,1)S(1)} %copy-done, f32[8,128]{1,0:T(8,128)S(1)} %pad_maximum_fusion.2.meta_ref, ...), custom_call_target="tpu_custom_call" | custom-call | tf_op jit(solution)/shard_map/pallas_call | solution.py:133
  74.7 0.0 copy-start.10
  74.8 0.1 fusion.12
  74.9 4.3 %convolution_bitcast_fusion.1 = f32[512,256]{0,1:T(8,128)S(1)} fusion(bf16[4096,256]{1,0:T(8,128)(2,1)} %bitcast.52, bf16[512,4096]{1,0:T(8,128)(2,1)} %bitcast.58), kind=kOutput, calls=%fused_computation.8 | convolution fusion | flops 1073741824 | bytes 6815744 | tf_op jit(solution)/shard_map/dot_general | solution.py:208
  79.2 1.3 convolution_bitcast_fusion
  80.5 0.3 select_reduce_fusion.1
  80.8 0.5 copy-done.5
  81.3 1.4 multiply_convert_fusion
  82.8 0.1 copy-done.12
  82.9 2.5 multiply_reduce_fusion
  85.5 0.7 copy-done.7
  86.2 0.2 copy.17
  86.4 0.4 convolution_convert_fusion.2
  86.8 1.3 fusion.3
  88.1 0.3 copy-done.6
  88.4 3.3 %add_convert_fusion = bf16[512,4096]{1,0:T(8,128)(2,1)} fusion(f32[512,4096]{1,0:T(8,128)S(1)} %fusion.3, bf16[4096,256]{1,0:T(8,128)(2,1)S(1)} %bitcast.53, bf16[512,512]{1,0:T(8,128)(2,1)S(1)} %bitcast.55), kind=kOutput, calls=%fused_computation | convolution fusion | flops 1077936128 | bytes 14942208 | tf_op jit(solution)/shard_map/dot_general | solution.py:165
  91.6 0.0 reduce-scatter.4.cloned.1.call-update
  91.7 0.0 reduce-scatter.6.cloned.1.call-start
  91.7 50.6 %reduce-scatter.4.cloned.1.call-done = bf16[512,2048]{1,0:T(8,128)(2,1)} async-done(((bf16[512,4096]{1,0:T(8,128)(2,1)}), bf16[512,2048]{1,0:T(8,128)(2,1)}) %reduce-scatter.4.cloned.1.call-update) | async-done | bytes 2097168 | tf_op jit(solution)/shard_map/reduce_scatter | solution.py:229
  142.4 0.0 reduce-scatter.6.cloned.1.call-update
  142.4 0.2 reduce-scatter.8.cloned.1.call-start
  142.6 0.0 copy-start.8
  142.6 3.6 %convolution_convert_fusion.1 = bf16[4096,256]{0,1:T(8,128)(2,1)S(1)} fusion(bf16[512,256]{0,1:T(8,128)(2,1)S(1)} %copy-done.13, bf16[512,4096]{1,0:T(8,128)(2,1)} %bitcast.51), kind=kOutput, calls=%fused_computation.5 | convolution fusion | flops 1074790400 | bytes 6553600 | tf_op jit(solution)/shard_map/dot_general | solution.py:159
  146.3 2.3 fusion
  148.6 3.4 %pad_maximum_fusion = bf16[4096,768]{0,1:T(8,128)(2,1)} fusion(bf16[4096,256]{0,1:T(8,128)(2,1)S(1)} %convolution_convert_fusion.1, bf16[4096,512]{0,1:T(8,128)(2,1)S(1)} %fusion), kind=kLoop, calls=%fused_computation.2 | loop fusion | flops 12582912 | bytes 12582912 | tf_op jit(solution)/shard_map/concatenate | solution.py:246
  152.0 0.0 reduce-scatter.8.cloned.1.call-update
  152.1 0.0 all-gather.2.cloned.1.call-start
  152.1 36.5 %reduce-scatter.6.cloned.1.call-done = bf16[128,2048]{1,0:T(8,128)(2,1)} async-done(((bf16[512,2048]{1,0:T(8,128)(2,1)}), bf16[128,2048]{1,0:T(8,128)(2,1)}) %reduce-scatter.6.cloned.1.call-update) | async-done | bytes 524304 | tf_op jit(solution)/shard_map/reduce_scatter | solution.py:232
  188.6 0.0 all-gather.2.cloned.1.call-update
  188.7 0.3 select_reduce_fusion
  189.0 19.4 %psum.7 = f32[4,2,128]{2,1,0:T(2,128)S(1)} all-reduce(f32[4,2,128]{2,1,0:T(2,128)S(1)} %broadcast_select_fusion), channel_id=1, replica_groups=mesh['ep'=4,'fsdp'=4,'tp'=2] {'ep','tp'}, use_global_device_ids=true, to_apply=%region_9.10 | all-reduce | flops 1024 | bytes 8192 | tf_op jit(solution)/shard_map/psum | solution.py:239
  208.4 0.6 bitcast_subtract_fusion
  209.0 38.9 %reduce-scatter.8.cloned.1.call-done = bf16[1024,768]{0,1:T(8,128)(2,1)} async-done(((bf16[4096,768]{0,1:T(8,128)(2,1)}), bf16[1024,768]{0,1:T(8,128)(2,1)}) %reduce-scatter.8.cloned.1.call-update) | async-done | bytes 1572880 | tf_op jit(solution)/shard_map/reduce_scatter | solution.py:247
  247.9 1.8 convert_element_type.50
  249.7 1.2 slice_bitcast_fusion
  250.9 1.3 copy.15
  252.2 1.3 copy.14
  253.5 17.0 %all-gather.2.cloned.1.call-done = bf16[128,4096]{1,0:T(8,128)(2,1)} async-done(((bf16[128,2048]{1,0:T(8,128)(2,1)}), bf16[128,4096]{1,0:T(8,128)(2,1)}) %all-gather.2.cloned.1.call-update) | async-done | bytes 1048592 | tf_op jit(solution)/shard_map/all_gather | solution.py:233
  270.5 2.3 copy.19
  (25 shorter events, 0.1 us)
Async XLA Ops:
  7.2 135.2 %reduce-scatter.4.cloned.1.call-start = ((), (), s32[]{:S(2)}) async-start(), calls=%async_computation.3 | async-start | bytes 6291456 | tf_op jit(solution)/shard_map/reduce_scatter | solution.py:229
  10.0 1.2 copy-start
  11.2 1.0 copy-start.1
  12.3 1.0 copy-start.2
  13.3 1.0 copy-start.3
  74.7 4.5 %copy-start.10 = (bf16[1,4,1,128,4096]{4,3,2,1,0:T(8,128)(2,1)S(1)}, bf16[1,4,1,128,4096]{4,3,2,1,0:T(8,128)(2,1)}, u32[]{:S(2)}) copy-start(bf16[1,4,1,128,4096]{4,3,2,1,0:T(8,128)(2,1)} %param.10) | copy-start | bytes 12582916
  79.2 2.2 copy-start.5
  81.3 1.6 copy-start.12
  82.8 2.7 copy-start.4
  85.5 0.7 copy-start.7
  86.8 1.6 copy-start.6
  91.6 51.0 %copy-start.13 = (bf16[512,256]{0,1:T(8,128)(2,1)S(1)}, bf16[512,256]{0,1:T(8,128)(2,1)}, u32[]{:S(2)}) copy-start(bf16[512,256]{0,1:T(8,128)(2,1)} %get-tuple-element.23) | copy-start | bytes 786436
  91.7 97.0 %reduce-scatter.6.cloned.1.call-start = ((), (), s32[]{:S(2)}) async-start(), calls=%async_computation.4 | async-start | bytes 2621440 | tf_op jit(solution)/shard_map/reduce_scatter | solution.py:232
  142.4 105.5 %reduce-scatter.8.cloned.1.call-start = ((), (), s32[]{:S(2)}) async-start(), calls=%async_computation.6 | async-start | bytes 7864320 | tf_op jit(solution)/shard_map/reduce_scatter | solution.py:247
  142.6 3.6 %copy-start.8 = (bf16[512,256]{0,1:T(8,128)(2,1)S(1)}, bf16[512,256]{0,1:T(8,128)(2,1)}, u32[]{:S(2)}) copy-start(bf16[512,256]{0,1:T(8,128)(2,1)} %copy-done.7) | copy-start | bytes 786436
  142.6 3.6 %copy-start.11 = (bf16[1,4,1,128,4096]{4,3,2,1,0:T(8,128)(2,1)S(1)}, bf16[1,4,1,128,4096]{4,3,2,1,0:T(8,128)(2,1)}, u32[]{:S(2)}) copy-start(bf16[1,4,1,128,4096]{4,3,2,1,0:T(8,128)(2,1)} %param.10) | copy-start | bytes 12582916
  152.0 56.4 %copy-start.9 = (f32[128,2]{0,1:T(2,128)S(1)}, f32[128,2]{0,1:T(2,128)}, u32[]{:S(2)}) copy-start(f32[128,2]{0,1:T(2,128)} %param.9) | copy-start | bytes 3076
  152.1 118.5 %all-gather.2.cloned.1.call-start = ((), (), s32[]{:S(2)}) async-start(), calls=%async_computation.5 | async-start | bytes 1572864 | tf_op jit(solution)/shard_map/all_gather | solution.py:233
Sparse Core Ops, SparseCore 0:
  91.8 50.5 reduce-scatter.3
  144.6 43.9 reduce-scatter.5
  191.2 56.6 reduce-scatter.7
  249.3 21.1 all-gather.1
